TPU v7x, 32 devices: a whole 2x2x4 slice. The times are simulated.
32 devices in a mesh: ep: 8 (over z, y), tp: 4 (over x, core).
Axes of the slice: x: 2, y: 2, z: 4, core: 2. Of those that a mesh axis runs over, the one named last changes fastest.
Arguments:
- tokens: bfloat16 [512, 4096], P(('ep', 'tp')), may hold values from -6 to 6
- routes: int32 [512, 2], P(('ep', 'tp')), may hold values from 0 to 7, all different within a row; in each aligned block of 16 rows (0 to 15, 16 to 31, ...) at most 8 rows name the same one
- combine: float32 [512, 2], P(('ep', 'tp')), may hold values from 0.25 to 1
- gate_weight: bfloat16 [8, 4096, 4096], P('ep', None, 'tp'), may hold values from -0.09375 to 0.09375
- up_weight: bfloat16 [8, 4096, 4096], P('ep', None, 'tp'), may hold values from -0.09375 to 0.09375
- down_weight: bfloat16 [8, 4096, 4096], P('ep', 'tp'), may hold values from -0.09375 to 0.09375
Outputs:
- moe_output: bfloat16 [512, 4096], P(('ep', 'tp'))
Inputs may be any that keep to these rules, and one draw needn't show every extreme that they name: `routes`: each row names 2 different experts. Among the rows of one device no expert is named more than 8 times, and in every draw some expert is named exactly 8 times by the rows of some device.
All inputs are finite; a program needn't handle non-finite values.
Results may differ from a plain program's by a relative error of at most 0.015.
Values may be sent and summed in bfloat16 or wider, within the bound.
A program may use at most 64 MiB of HBM per device.

v0:
```python
import jax
import jax.numpy as jnp
from jax import lax
from jax.sharding import PartitionSpec as P


def body(tokens, routes, combine, gate_weight, up_weight, down_weight):
    token_rows, feature_width = tokens.shape
    top_count = routes.shape[1]
    experts_here = gate_weight.shape[0]
    rank_count = lax.axis_size("ep")
    experts_all = experts_here * rank_count
    capacity = 2 * token_rows * top_count // experts_all
    flat_ids = routes.reshape(-1)
    onehot = (flat_ids[:, None] == jnp.arange(experts_all, dtype=jnp.int32)[None, :]).astype(
        jnp.int32
    )
    earlier = jnp.cumsum(onehot, axis=0) - onehot
    slot_index = jnp.sum(earlier * onehot, axis=1)
    target = flat_ids * capacity + slot_index
    selector = (
        target[:, None] == jnp.arange(experts_all * capacity, dtype=jnp.int32)[None, :]
    ).astype(jnp.bfloat16)
    repeated = jnp.repeat(tokens, top_count, axis=0)
    buffer = lax.dot_general(
        selector, repeated, (((0,), (0,)), ((), ())), preferred_element_type=jnp.float32
    ).astype(jnp.bfloat16)
    shaped = buffer.reshape(rank_count, 1, experts_here, capacity, feature_width)
    arrived = lax.all_to_all(shaped, "ep", split_axis=0, concat_axis=0, tiled=True)
    block_rows = lax.all_gather(arrived, "tp", axis=1, tiled=True)
    gate_values = jnp.einsum(
        "abecd,edf->abecf", block_rows, gate_weight, preferred_element_type=jnp.float32
    )
    up_values = jnp.einsum(
        "abecd,edf->abecf", block_rows, up_weight, preferred_element_type=jnp.float32
    )
    hidden = (jax.nn.silu(gate_values) * up_values).astype(jnp.bfloat16)
    partials = jnp.einsum(
        "abecf,efd->abecd", hidden, down_weight, preferred_element_type=jnp.float32
    )
    summed = lax.psum_scatter(partials.astype(jnp.bfloat16), "tp", scatter_dimension=1, tiled=True)
    returned = lax.all_to_all(summed, "ep", split_axis=0, concat_axis=0, tiled=True)
    returned = returned.reshape(experts_all * capacity, feature_width)
    picked = jnp.dot(selector, returned, preferred_element_type=jnp.float32).reshape(
        token_rows, top_count, feature_width
    )
    return jnp.sum(combine[:, :, None] * picked, axis=1).astype(jnp.bfloat16)


def solution(mesh):
    return jax.shard_map(
        body,
        mesh=mesh,
        in_specs=(
            P(("ep", "tp"), None),
            P(("ep", "tp"), None),
            P(("ep", "tp"), None),
            P("ep", None, "tp"),
            P("ep", None, "tp"),
            P("ep", "tp", None),
        ),
        out_specs=P(("ep", "tp"), None),
        check_vma=False,
    )
```

profile of v0, /device:TPU:0, one launch (start us, length us, event | category | flops | bytes accessed | tf_op | source)
XLA Modules:
  0.0 152.7 jit_solution(6297224300718134010)
XLA Ops:
  6.5 0.8 copy.24
  7.3 0.1 eq.50
  7.4 0.1 fusion.52
  7.5 0.1 reduce_window_sum.11
  7.5 0.2 select_reduce_fusion
  7.7 1.1 broadcast_in_dim.2
  8.8 0.1 reshape.65
  8.9 0.4 fusion.12
  9.3 21.7 %all_to_all.10 = bf16[8,1,1,8,4096]{4,3,1,2,0:T(8,128)(2,1)} all-to-all(bf16[8,1,1,8,4096]{4,3,1,2,0:T(8,128)(2,1)S(1)} %fusion.12), channel_id=1, replica_groups=mesh['ep'=8,'tp'=4] {'ep'}, dimensions={0} | all-to-all | bytes 1048576 | tf_op jit(solution)/shard_map/all_to_all | solution.py:29
  31.1 0.0 all-gather.2.cloned.1.call-update
  31.1 0.0 all-reduce.3.cloned.1.call-start
  31.2 21.7 %all-gather.2.cloned.1.call-done = bf16[8,4,1,8,4096]{4,3,1,0,2:T(8,128)(2,1)} async-done(((bf16[8,1,1,8,4096]{4,3,1,0,2:T(8,128)(2,1)}), bf16[8,4,1,8,4096]{4,3,1,0,2:T(8,128)(2,1)}) %all-gather.2.cloned.1.call-update) | async-done | bytes 2097168 | tf_op jit(solution)/shard_map/all_gather | solution.py:30
  52.8 6.5 %fusion.15 = f32[8,4,1,8,1024]{4,3,1,0,2:T(8,128)S(1)} fusion(bf16[1,4096,1024]{2,1,0:T(8,128)(2,1)} %param.9, bf16[8,4,1,8,4096]{4,3,1,0,2:T(8,128)(2,1)} %all-gather.2.cloned.1.call-done), kind=kOutput, calls=%fused_computation.13 | convolution fusion | flops 2147483648 | bytes 11534336 | tf_op jit(solution)/shard_map/abecd,edf->abecf/dot_general | solution.py:31
  59.3 0.0 copy-start.3
  59.4 11.7 %fusion.9 = bf16[8,4,1,8,4096]{4,3,1,0,2:T(8,128)(2,1)} fusion(bf16[1,1024,4096]{2,1,0:T(8,128)(2,1)} %param.11, bf16[1,4096,1024]{2,1,0:T(8,128)(2,1)} %param.10, bf16[8,4,1,8,4096]{4,3,1,0,2:T(8,128)(2,1)S(1)} %copy-done.2, f32[8,4,1,8,1024]{4,3,1,0,2:T(8,128)S(1)} %fusion.15), kind=kOutput, calls=%fused_computation.7 | convolution fusion | flops 4297588736 | bytes 22020096 | tf_op jit(solution)/shard_map/abecf,efd->abecd/dot_general | solution.py:38
  71.0 0.0 all-reduce.3.cloned.1.call-update
  71.1 0.6 dynamic-slice
  71.7 50.9 %all-reduce.3.cloned.1.call-done = bf16[8,4,1,8,4096]{4,3,1,0,2:T(8,128)(2,1)} async-done(((bf16[8,4,1,8,4096]{4,3,1,0,2:T(8,128)(2,1)}), bf16[8,4,1,8,4096]{4,3,1,0,2:T(8,128)(2,1)}) %all-reduce.3.cloned.1.call-update) | async-done | bytes 2097168
  122.6 2.5 %dynamic-slice_bitcast_fusion = bf16[8,1,1,8,4096]{4,3,1,2,0:T(8,128)(2,1)} fusion(bf16[8,4,1,8,4096]{4,3,1,0,2:T(8,128)(2,1)} %all-reduce.3.cloned.1.call-done, u32[]{:T(128)} %bitcast.44), kind=kLoop, calls=%fused_computation.25 | loop fusion | bytes 1048580 | tf_op jit(solution)/shard_map/reduce_scatter | solution.py:41
  125.1 5.5 %all-to-all-start.1 = ((bf16[8,1,1,8,4096]{4,3,1,2,0:T(8,128)(2,1)}), bf16[8,1,1,8,4096]{4,3,1,2,0:T(8,128)(2,1)S(1)}, u32[]{:S(2)}, u32[]{:S(2)}) async-start(bf16[8,1,1,8,4096]{4,3,1,2,0:T(8,128)(2,1)} %dynamic-slice_bitcast_fusion), calls=%async_computation.1 | async-start | bytes 1048576 | tf_op jit(solution)/shard_map/all_to_all | solution.py:42
  130.6 0.1 reduce_sum.21
  130.7 0.1 copy.25
  130.8 14.1 %all-to-all-done.1 = bf16[8,1,1,8,4096]{4,3,1,2,0:T(8,128)(2,1)S(1)} async-done(((bf16[8,1,1,8,4096]{4,3,1,2,0:T(8,128)(2,1)}), bf16[8,1,1,8,4096]{4,3,1,2,0:T(8,128)(2,1)S(1)}, u32[]{:S(2)}, u32[]{:S(2)}) %all-to-all-start.1) | async-done | bytes 524320 | tf_op jit(solution)/shard_map/all_to_all | solution.py:42
  144.9 0.9 fusion.44
  (10 shorter events, 0.0 us)
Async XLA Ops:
  6.5 46.3 %all-gather.2.cloned.1.call-start = ((), (), s32[]{:S(2)}) async-start(), calls=%async_computation.2 | async-start | bytes 2621440 | tf_op jit(solution)/shard_map/all_gather | solution.py:30
  31.1 91.5 %all-reduce.3.cloned.1.call-start = ((), (), s32[]{:S(2)}) async-start(), calls=%async_computation.3 | async-start | bytes 4194304
  52.8 6.5 %copy-start.2 = (bf16[8,4,1,8,4096]{4,3,1,0,2:T(8,128)(2,1)S(1)}, bf16[8,4,1,8,4096]{4,3,1,0,2:T(8,128)(2,1)}, u32[]{:S(2)}) copy-start(bf16[8,4,1,8,4096]{4,3,1,0,2:T(8,128)(2,1)} %all-gather.2.cloned.1.call-done) | copy-start | bytes 6291460
  59.3 11.7 %copy-start.3 = (u32[32]{0:T(128)S(1)}, u32[32]{0:T(128)}, u32[]{:S(2)}) copy-start(u32[32]{0:T(128)} %constant.21) | copy-start | bytes 388
  59.4 71.4 %copy-start = (s32[16,2]{0,1:T(2,128)S(1)}, s32[16,2]{0,1:T(2,128)}, u32[]{:S(2)}) copy-start(s32[16,2]{0,1:T(2,128)} %param.7) | copy-start | bytes 388
  59.4 85.5 %copy-start.1 = (f32[16,2]{0,1:T(2,128)S(1)}, f32[16,2]{0,1:T(2,128)}, u32[]{:S(2)}) copy-start(f32[16,2]{0,1:T(2,128)} %param.8) | copy-start | bytes 388
  125.1 19.8 %all-to-all-start.1 = ((bf16[8,1,1,8,4096]{4,3,1,2,0:T(8,128)(2,1)}), bf16[8,1,1,8,4096]{4,3,1,2,0:T(8,128)(2,1)S(1)}, u32[]{:S(2)}, u32[]{:S(2)}) async-start(bf16[8,1,1,8,4096]{4,3,1,2,0:T(8,128)(2,1)} %dynamic-slice_bitcast_fusion), calls=%async_computation.1 | async-start | bytes 1048576 | tf_op jit(solution)/shard_map/all_to_all | solution.py:42
Sparse Core Ops, SparseCore 0:
  31.2 21.5 all-gather.1
  71.2 51.3 all-reduce.2
where the time goes:
time: 153 us
  waiting for transfers between devices  86.7 us (57%)
  blocking collectives  21.7 us (14%)
  matrix products  19.5 us (13%)
  between operations  13.5 us (9%)
  starting transfers between devices  5.56 us (4%)
  local copies, waits for them, and re-layouts  5.33 us (3%)
    unnamed x3, waiting for transfers between devices  51 us
    all_to_all x1, blocking collectives, body(): lax.all_to_all(shaped, 'ep', split_axis=0, concat_axis=0, tiled=True)  21.7 us
    all_gather x1, waiting for transfers between devices, body(): block_rows = lax.all_gather(arrived, 'tp', axis=1, tiled=True)  21.7 us
    all_to_all x1, waiting for transfers between devices, body(): lax.all_to_all(summed, 'ep', split_axis=0, concat_axis=0, tiled=True)  14.1 us
    dot_general x1, matrix products, body(): jnp.einsum('abecf,efd->abecd', hidden, down_weight, preferred_element_typ...  11.7 us
    dot_general x1, matrix products, body(): jnp.einsum('abecd,edf->abecf', block_rows, gate_weight, preferred_element...  6.49 us
    all_to_all x1, starting transfers between devices, body(): lax.all_to_all(summed, 'ep', split_axis=0, concat_axis=0, tiled=True)  5.52 us
  transfers between devices with their start and end apart: 3, of which 3 were waited for; matrix products, arithmetic and copies ran while one was open for 0% of the time, Pallas kernels for 0%

commit v1 on v0

v1 whole, which is shorter than its diff:
```python
import functools
import jax
import jax.numpy as jnp
from jax import lax
from jax.experimental import pallas as pl
from jax.experimental.pallas import tpu as pltpu
from jax.sharding import PartitionSpec as P

MESH = pl.DeviceIdType.MESH
F32, BF16 = jnp.float32, jnp.bfloat16


def kernel(
    tokens_ref, routes_ref, combine_ref, gate_hbm, up_hbm, down_hbm, out_ref,
    gate_ref, up_ref, down_ref, slots, rows, gate_acc, up_acc, hidden,
    part, pair, summed, across, ready, back, weights,
    w_sem, a_send, a_recv, x_send, x_recv, d_send, d_recv,
    q_send, q_recv, t_send, t_recv, v_send, v_recv,
    *, experts, capacity, pad,
):
    token_rows, width = tokens_ref.shape
    chunks, cut = rows.shape[0], rows.shape[-1]
    sides = rows.shape[2]
    inner = gate_ref.shape[-1]
    all_rows = 2 * sides * experts * pad
    me = lax.axis_index("ep")
    tp = lax.axis_index("tp")
    core = lax.rem(tp, 2)
    side = lax.div(tp, 2)
    mate = 1 - core

    def ep_peer(i):
        return lax.rem(me + i, experts)

    def side_peer(i):
        return lax.rem(side + i, sides)

    def at_ep(e):
        return {"ep": e, "tp": tp}

    def at_side(s):
        return {"ep": me, "tp": s * 2 + core}

    at_mate = {"ep": me, "tp": side * 2 + mate}

    def remote(src, dst, send, recv, target):
        return pltpu.make_async_remote_copy(
            src_ref=src, dst_ref=dst, send_sem=send, recv_sem=recv,
            device_id=target, device_id_type=MESH,
        )

    def weight_copies(k):
        span = pl.ds(pl.multiple_of(k * cut, cut), cut)
        return (
            pltpu.make_async_copy(gate_hbm.at[0, span, :], gate_ref.at[k], w_sem.at[0, k]),
            pltpu.make_async_copy(up_hbm.at[0, span, :], up_ref.at[k], w_sem.at[1, k]),
        )

    def down_copy(k):
        span = pl.ds(pl.multiple_of(k * cut, cut), cut)
        return pltpu.make_async_copy(down_hbm.at[0, :, span], down_ref.at[k], w_sem.at[2, k])

    barrier = pltpu.get_barrier_semaphore()
    for i in range(1, experts):
        pl.semaphore_signal(barrier, inc=1, device_id=at_ep(ep_peer(i)), device_id_type=MESH)
    for i in range(1, sides):
        pl.semaphore_signal(barrier, inc=1, device_id=at_side(side_peer(i)), device_id_type=MESH)
    pl.semaphore_signal(barrier, inc=1, device_id=at_mate, device_id_type=MESH)

    for k in range(chunks):
        for copy in weight_copies(k):
            copy.start()

    column = lax.broadcasted_iota(jnp.int32, (token_rows, experts * pad), 1)
    column_expert, column_slot = lax.div(column, pad), lax.rem(column, pad)
    first = routes_ref[:, 0:1] == column_expert
    second = routes_ref[:, 1:2] == column_expert
    named = jnp.where(first, 1.0, 0.0) + jnp.where(second, 1.0, 0.0)
    row_at = lax.broadcasted_iota(jnp.int32, (token_rows, token_rows), 0)
    row_of = lax.broadcasted_iota(jnp.int32, (token_rows, token_rows), 1)
    before = jnp.where(row_of < row_at, 1.0, 0.0)
    earlier = jnp.dot(before.astype(BF16), named.astype(BF16), preferred_element_type=F32)
    taken = earlier == column_slot.astype(F32)
    selector = jnp.where(taken, named, 0.0).astype(BF16)
    share = jnp.where(first, combine_ref[:, 0:1], 0.0) + jnp.where(second, combine_ref[:, 1:2], 0.0)
    share = jnp.where(taken, share, 0.0)
    share_high = share.astype(BF16)
    weights[0:token_rows, :] = share_high.astype(F32)
    weights[token_rows : 2 * token_rows, :] = share - share_high.astype(F32)

    pl.semaphore_wait(barrier, experts - 1 + sides)

    def a_copy(k, e):
        return remote(
            slots.at[k, e], rows.at[k, core, side, me], a_send.at[k, e], a_recv.at[k, me], at_ep(e)
        )

    for k in range(chunks):
        block = lax.dot_general(
            selector, tokens_ref[:, k * cut : (k + 1) * cut],
            (((0,), (0,)), ((), ())), preferred_element_type=F32,
        )
        slots[k] = block.reshape(experts, pad, cut).astype(BF16)
        for i in range(1, experts):
            a_copy(k, ep_peer(i)).start()
        rows[k, core, side, me] = slots[k, me]
    for k in range(chunks):
        down_copy(k).start()

    def x_copy(k, s):
        return remote(
            rows.at[k, core, side], rows.at[k, core, side],
            x_send.at[k, s], x_recv.at[k, side], at_side(s),
        )

    def d_copy(k, s):
        return remote(
            rows.at[k, core, s], rows.at[k, core, s], d_send.at[k, s], d_recv.at[k, s], at_mate
        )

    gate_acc[...] = jnp.zeros_like(gate_acc)
    up_acc[...] = jnp.zeros_like(up_acc)

    def dispatch(step, carry):
        @pl.when(step < chunks)
        def _():
            k = step
            for i in range(1, experts):
                e = ep_peer(i)
                remote(
                    slots.at[k, e], rows.at[k, core, side, e],
                    a_send.at[k, e], a_recv.at[k, e], at_ep(e),
                ).wait_recv()
            for i in range(1, sides):
                x_copy(k, side_peer(i)).start()
            d_copy(k, side).start()

        @pl.when(jnp.logical_and(step >= 1, step < chunks + 1))
        def _():
            k = step - 1
            for i in range(1, sides):
                s = side_peer(i)
                remote(
                    rows.at[k, core, s], rows.at[k, core, s],
                    x_send.at[k, s], x_recv.at[k, s], at_side(s),
                ).wait_recv()
                d_copy(k, s).start()

        @pl.when(step >= 2)
        def _():
            k = step - 2
            for copy in weight_copies(k):
                copy.wait()
            for s in range(sides):
                remote(
                    rows.at[k, mate, s], rows.at[k, mate, s],
                    d_send.at[k, s], d_recv.at[k, s], at_mate,
                ).wait_recv()
            x = rows[k].astype(F32).reshape(all_rows, cut).astype(BF16)
            gate_acc[...] += jnp.dot(x, gate_ref[k], preferred_element_type=F32)
            up_acc[...] += jnp.dot(x, up_ref[k], preferred_element_type=F32)

        return carry

    lax.fori_loop(0, chunks + 2, dispatch, 0)

    gates = gate_acc[...]
    hidden[...] = (gates / (1.0 + jnp.exp(-gates)) * up_acc[...]).astype(BF16)

    def q_copy(k):
        return remote(part.at[k, mate], pair.at[k], q_send.at[k], q_recv.at[k], at_mate)

    def t_copy(k, s):
        return remote(
            summed.at[k, s], across.at[k, side], t_send.at[k, s], t_recv.at[k, side], at_side(s)
        )

    def v_copy(k, e):
        return remote(ready.at[k, e], back.at[k, me], v_send.at[k, e], v_recv.at[k, me], at_ep(e))

    def down(step, carry):
        @pl.when(step < chunks)
        def _():
            k = step
            down_copy(k).wait()
            block = jnp.dot(hidden[...], down_ref[k], preferred_element_type=F32)
            part[k] = block.reshape(2, sides, experts, pad, cut).astype(BF16)
            q_copy(k).start()

        @pl.when(step >= 2)
        def _():
            k = step - 2
            q_copy(k).wait_recv()
            for i in range(1, sides):
                s = side_peer(i)
                summed[k, s] = (part[k, core, s].astype(F32) + pair[k, s].astype(F32)).astype(BF16)
                t_copy(k, s).start()

        return carry

    lax.fori_loop(0, chunks + 2, down, 0)

    share_rows = weights[...].astype(BF16)

    def finish(step, carry):
        @pl.when(step < chunks)
        def _():
            k = step
            total = part[k, core, side].astype(F32) + pair[k, side].astype(F32)
            for i in range(1, sides):
                s = side_peer(i)
                remote(
                    summed.at[k, s], across.at[k, s],
                    t_send.at[k, s], t_recv.at[k, s], at_side(s),
                ).wait_recv()
                total = total + across[k, s].astype(F32)
            ready[k] = total.astype(BF16)
            for i in range(1, experts):
                v_copy(k, ep_peer(i)).start()
            back[k, me] = ready[k, me]

        @pl.when(step >= 1)
        def _():
            k = step - 1
            for i in range(1, experts):
                e = ep_peer(i)
                remote(
                    ready.at[k, e], back.at[k, e], v_send.at[k, e], v_recv.at[k, e], at_ep(e)
                ).wait_recv()
            returned = back[k].astype(F32).reshape(experts * pad, cut).astype(BF16)
            both = jnp.dot(share_rows, returned, preferred_element_type=F32)
            span = pl.ds(pl.multiple_of(k * cut, cut), cut)
            out_ref[:, span] = (both[:token_rows] + both[token_rows:]).astype(BF16)

        return carry

    lax.fori_loop(0, chunks + 1, finish, 0)

    def drain(k, carry):
        for i in range(1, experts):
            a_copy(k, ep_peer(i)).wait_send()
            v_copy(k, ep_peer(i)).wait_send()
        for i in range(1, sides):
            x_copy(k, side_peer(i)).wait_send()
            t_copy(k, side_peer(i)).wait_send()
        for s in range(sides):
            d_copy(k, s).wait_send()
        q_copy(k).wait_send()
        return carry

    lax.fori_loop(0, chunks, drain, 0)


def body(tokens, routes, combine, gate_weight, up_weight, down_weight):
    token_rows, width = tokens.shape
    top = routes.shape[1]
    inner = gate_weight.shape[-1]
    experts = lax.axis_size("ep")
    sides = lax.axis_size("tp") // 2
    capacity = 2 * token_rows * top // experts
    pad = -(-capacity // 8) * 8
    cut = min(512, width)
    chunks = width // cut
    all_rows = 2 * sides * experts * pad
    vmem, dma = pltpu.VMEM, pltpu.SemaphoreType.DMA
    in_vmem = pl.BlockSpec(memory_space=pltpu.VMEM)
    in_hbm = pl.BlockSpec(memory_space=pl.ANY)
    group = (experts, pad, cut)
    return pl.pallas_call(
        functools.partial(kernel, experts=experts, capacity=capacity, pad=pad),
        out_shape=jax.ShapeDtypeStruct((token_rows, width), BF16),
        in_specs=[in_vmem] * 3 + [in_hbm] * 3,
        out_specs=in_vmem,
        scratch_shapes=[
            vmem((chunks, cut, inner), BF16),
            vmem((chunks, cut, inner), BF16),
            vmem((chunks, inner, cut), BF16),
            vmem((chunks,) + group, BF16),
            vmem((chunks, 2, sides) + group, BF16),
            vmem((all_rows, inner), F32),
            vmem((all_rows, inner), F32),
            vmem((all_rows, inner), BF16),
            vmem((chunks, 2, sides) + group, BF16),
            vmem((chunks, sides) + group, BF16),
            vmem((chunks, sides) + group, BF16),
            vmem((chunks, sides) + group, BF16),
            vmem((chunks,) + group, BF16),
            vmem((chunks,) + group, BF16),
            vmem((2 * token_rows, experts * pad), F32),
            dma((3, chunks)),
            dma((chunks, experts)), dma((chunks, experts)),
            dma((chunks, sides)), dma((chunks, sides)),
            dma((chunks, sides)), dma((chunks, sides)),
            dma((chunks,)), dma((chunks,)),
            dma((chunks, sides)), dma((chunks, sides)),
            dma((chunks, experts)), dma((chunks, experts)),
        ],
        compiler_params=pltpu.CompilerParams(
            collective_id=0, has_side_effects=True, vmem_limit_bytes=60 * 1024 * 1024
        ),
    )(tokens, routes, combine, gate_weight, up_weight, down_weight)


def solution(mesh):
    return jax.shard_map(
        body,
        mesh=mesh,
        in_specs=(
            P(("ep", "tp"), None),
            P(("ep", "tp"), None),
            P(("ep", "tp"), None),
            P("ep", None, "tp"),
            P("ep", None, "tp"),
            P("ep", "tp", None),
        ),
        out_specs=P(("ep", "tp"), None),
        check_vma=False,
    )
```

time: 153 us -> 65.3 us (0.43)
  waiting for transfers between devices: 86.7 us -> 0 us
  Pallas kernels: 0 us -> 60.9 us
  blocking collectives: 21.7 us -> 0 us
  matrix products: 19.5 us -> 0 us
  between operations: 13.5 us -> 0.01 us
  starting transfers between devices: 5.56 us -> 0 us
    pallas_call x0 -> x1, Pallas kernels: none -> 60.9 us  [body(): pl.pallas_call(functools.partial(kernel, experts=experts, capacity=capaci...]
    unnamed x3 -> x0, waiting for transfers between devices: 51 us -> none
    all_to_all x1 -> x0, blocking collectives: 21.7 us -> none  [body(): lax.all_to_all(shaped, 'ep', split_axis=0, concat_axis=0, tiled=True)]
    all_gather x1 -> x0, waiting for transfers between devices: 21.7 us -> none  [body(): block_rows = lax.all_gather(arrived, 'tp', axis=1, tiled=True)]
    dot_general x4 -> x0, matrix products: 19.5 us -> none  [the longest x1 11.7 us: body(): jnp.einsum('abecf,efd->abecd', hidden, down_weight, preferred_element_typ...]
    all_to_all x1 -> x0, waiting for transfers between devices: 14.1 us -> none  [body(): lax.all_to_all(summed, 'ep', split_axis=0, concat_axis=0, tiled=True)]
    all_to_all x1 -> x0, starting transfers between devices: 5.52 us -> none  [body(): lax.all_to_all(summed, 'ep', split_axis=0, concat_axis=0, tiled=True)]
    unnamed x10 -> x3, local copies, waits for them, and re-layouts: 1.36 us -> 4.27 us
  transfers between devices with their start and end apart: 3 -> 0, of which waited for: 3 -> 0; matrix products, arithmetic and copies ran while one was open for 0% -> 0% of each run, Pallas kernels for 0% -> 0%
where the time goes in v1:
time: 65.3 us; the launch traced here: 65.1 us
  Pallas kernels  60.9 us (93%)
  local copies, waits for them, and re-layouts  4.27 us (7%)
    pallas_call x1, Pallas kernels, body(): pl.pallas_call(functools.partial(kernel, experts=experts, capacity=capaci...  60.9 us
    unnamed x3, local copies, waits for them, and re-layouts  4.27 us

profile of v1, /device:TPU:0, one launch (start us, length us, event | category | flops | bytes accessed | tf_op | source)
XLA Modules:
  0.0 65.1 jit_solution(1217952121795042433)
XLA Ops:
  0.0 1.4 %copy.7.routes_ref = s32[16,2]{1,0:T(8,128)} copy(s32[16,2]{0,1:T(2,128)} %param.7) | data formatting | bytes 256 | tf_op args[1]
  1.4 1.3 %copy.8.combine_ref = f32[16,2]{1,0:T(8,128)} copy(f32[16,2]{0,1:T(2,128)} %param.8) | data formatting | bytes 256 | tf_op args[2]
  2.7 60.9 %shard_map.64 = bf16[16,4096]{1,0:T(8,128)(2,1)} custom-call(bf16[16,4096]{1,0:T(8,128)(2,1)} %tokens_ref.1, s32[16,2]{1,0:T(8,128)} %copy.7.routes_ref, f32[16,2]{1,0:T(8,128)} %copy.8.combine_ref, bf16[1,4096,1024]{2,1,0:T(8,128)(2,1)} %gate_hbm.1, bf16[1,4096,1024]{2,1,0:T(8,128)(2,1)} %up_hbm.1, bf16[1,1024,4096]{2,1,0:T(8,128)(2,1)} %down_hbm.1), custom_call_target="tpu_custom_call" | custom-call | tf_op jit(solution)/shard_map/pallas_call | solution.py:269
  63.6 1.6 %copy.10 = bf16[16,4096]{1,0:T(8,128)(2,1)} copy(bf16[16,4096]{1,0:T(8,128)(2,1)} %shard_map.64) | data formatting | bytes 262144

commit v2 on v1

--- a/solution.py
+++ b/solution.py
@@ -29,8 +29,22 @@
     side = lax.div(tp, 2)
     mate = 1 - core
 
+    lanes = 2 if experts % 2 == 0 else 1
+    lines = experts // lanes
+    line, lane = lax.div(me, lanes), lax.rem(me, lanes)
+    far = sorted(range(1, lines), key=lambda d: (-min(d, lines - d), d)) + [0]
+    near = far[::-1]
+
+    def line_peer(d):
+        return lax.rem(line + d, lines)
+
+    def ep_at(d, b):
+        return line_peer(d) * lanes + lax.rem(lane + b, lanes)
+
+    ep_peers = [(d, b) for d in far for b in range(lanes) if (d, b) != (0, 0)]
+
     def ep_peer(i):
-        return lax.rem(me + i, experts)
+        return ep_at(*ep_peers[i - 1])
 
     def side_peer(i):
         return lax.rem(side + i, sides)
@@ -71,22 +85,22 @@
         for copy in weight_copies(k):
             copy.start()
 
-    column = lax.broadcasted_iota(jnp.int32, (token_rows, experts * pad), 1)
-    column_expert, column_slot = lax.div(column, pad), lax.rem(column, pad)
-    first = routes_ref[:, 0:1] == column_expert
-    second = routes_ref[:, 1:2] == column_expert
+    place = lax.broadcasted_iota(jnp.int32, (experts * pad, token_rows), 0)
+    place_expert, place_slot = lax.div(place, pad), lax.rem(place, pad)
+    first = routes_ref[0:1, :] == place_expert
+    second = routes_ref[1:2, :] == place_expert
     named = jnp.where(first, 1.0, 0.0) + jnp.where(second, 1.0, 0.0)
-    row_at = lax.broadcasted_iota(jnp.int32, (token_rows, token_rows), 0)
-    row_of = lax.broadcasted_iota(jnp.int32, (token_rows, token_rows), 1)
+    row_of = lax.broadcasted_iota(jnp.int32, (token_rows, token_rows), 0)
+    row_at = lax.broadcasted_iota(jnp.int32, (token_rows, token_rows), 1)
     before = jnp.where(row_of < row_at, 1.0, 0.0)
-    earlier = jnp.dot(before.astype(BF16), named.astype(BF16), preferred_element_type=F32)
-    taken = earlier == column_slot.astype(F32)
+    earlier = jnp.dot(named.astype(BF16), before.astype(BF16), preferred_element_type=F32)
+    taken = earlier == place_slot.astype(F32)
     selector = jnp.where(taken, named, 0.0).astype(BF16)
-    share = jnp.where(first, combine_ref[:, 0:1], 0.0) + jnp.where(second, combine_ref[:, 1:2], 0.0)
+    share = jnp.where(first, combine_ref[0:1, :], 0.0) + jnp.where(second, combine_ref[1:2, :], 0.0)
     share = jnp.where(taken, share, 0.0)
-    share_high = share.astype(BF16)
-    weights[0:token_rows, :] = share_high.astype(F32)
-    weights[token_rows : 2 * token_rows, :] = share - share_high.astype(F32)
+    share_high = share.astype(BF16).astype(F32)
+    weights[:, 0:token_rows] = share_high
+    weights[:, token_rows : 2 * token_rows] = share - share_high
 
     pl.semaphore_wait(barrier, experts - 1 + sides)
 
@@ -98,7 +112,7 @@
     for k in range(chunks):
         block = lax.dot_general(
             selector, tokens_ref[:, k * cut : (k + 1) * cut],
-            (((0,), (0,)), ((), ())), preferred_element_type=F32,
+            (((1,), (0,)), ((), ())), preferred_element_type=F32,
         )
         slots[k] = block.reshape(experts, pad, cut).astype(BF16)
         for i in range(1, experts):
@@ -107,16 +121,24 @@
     for k in range(chunks):
         down_copy(k).start()
 
-    def x_copy(k, s):
-        return remote(
-            rows.at[k, core, side], rows.at[k, core, side],
-            x_send.at[k, s], x_recv.at[k, side], at_side(s),
-        )
-
-    def d_copy(k, s):
-        return remote(
-            rows.at[k, core, s], rows.at[k, core, s], d_send.at[k, s], d_recv.at[k, s], at_mate
-        )
+    def row_block(k, c, s, z):
+        return rows.at[k, c, s, pl.ds(z * lanes, lanes)]
+
+    def x_copy(k, s, z):
+        block = row_block(k, core, side, z)
+        return remote(block, block, x_send.at[k, s, z], x_recv.at[k, side, z], at_side(s))
+
+    def x_arrival(k, s, z):
+        block = row_block(k, core, s, z)
+        return remote(block, block, x_send.at[k, s, z], x_recv.at[k, s, z], at_side(s))
+
+    def d_copy(k, s, z):
+        block = row_block(k, core, s, z)
+        return remote(block, block, d_send.at[k, s, z], d_recv.at[k, s, z], at_mate)
+
+    def d_arrival(k, s, z):
+        block = row_block(k, mate, s, z)
+        return remote(block, block, d_send.at[k, s, z], d_recv.at[k, s, z], at_mate)
 
     gate_acc[...] = jnp.zeros_like(gate_acc)
     up_acc[...] = jnp.zeros_like(up_acc)
@@ -125,26 +147,28 @@
         @pl.when(step < chunks)
         def _():
             k = step
-            for i in range(1, experts):
-                e = ep_peer(i)
-                remote(
-                    slots.at[k, e], rows.at[k, core, side, e],
-                    a_send.at[k, e], a_recv.at[k, e], at_ep(e),
-                ).wait_recv()
-            for i in range(1, sides):
-                x_copy(k, side_peer(i)).start()
-            d_copy(k, side).start()
+            for d in near:
+                z = line_peer(d)
+                for b in range(lanes):
+                    if (d, b) != (0, 0):
+                        e = ep_at(d, b)
+                        remote(
+                            slots.at[k, e], rows.at[k, core, side, e],
+                            a_send.at[k, e], a_recv.at[k, e], at_ep(e),
+                        ).wait_recv()
+                for i in range(1, sides):
+                    x_copy(k, side_peer(i), z).start()
+                d_copy(k, side, z).start()
 
         @pl.when(jnp.logical_and(step >= 1, step < chunks + 1))
         def _():
             k = step - 1
-            for i in range(1, sides):
-                s = side_peer(i)
-                remote(
-                    rows.at[k, core, s], rows.at[k, core, s],
-                    x_send.at[k, s], x_recv.at[k, s], at_side(s),
-                ).wait_recv()
-                d_copy(k, s).start()
+            for d in near:
+                z = line_peer(d)
+                for i in range(1, sides):
+                    s = side_peer(i)
+                    x_arrival(k, s, z).wait_recv()
+                    d_copy(k, s, z).start()
 
         @pl.when(step >= 2)
         def _():
@@ -152,10 +176,8 @@
             for copy in weight_copies(k):
                 copy.wait()
             for s in range(sides):
-                remote(
-                    rows.at[k, mate, s], rows.at[k, mate, s],
-                    d_send.at[k, s], d_recv.at[k, s], at_mate,
-                ).wait_recv()
+                for z in range(lines):
+                    d_arrival(k, s, z).wait_recv()
             x = rows[k].astype(F32).reshape(all_rows, cut).astype(BF16)
             gate_acc[...] += jnp.dot(x, gate_ref[k], preferred_element_type=F32)
             up_acc[...] += jnp.dot(x, up_ref[k], preferred_element_type=F32)
@@ -170,9 +192,18 @@
     def q_copy(k):
         return remote(part.at[k, mate], pair.at[k], q_send.at[k], q_recv.at[k], at_mate)
 
-    def t_copy(k, s):
+    def t_copy(k, s, z):
+        span = pl.ds(z * lanes, lanes)
         return remote(
-            summed.at[k, s], across.at[k, side], t_send.at[k, s], t_recv.at[k, side], at_side(s)
+            summed.at[k, s, span], across.at[k, side, span],
+            t_send.at[k, s, z], t_recv.at[k, side, z], at_side(s),
+        )
+
+    def t_arrival(k, s, z):
+        span = pl.ds(z * lanes, lanes)
+        return remote(
+            summed.at[k, s, span], across.at[k, s, span],
+            t_send.at[k, s, z], t_recv.at[k, s, z], at_side(s),
         )
 
     def v_copy(k, e):
@@ -194,29 +225,31 @@
             for i in range(1, sides):
                 s = side_peer(i)
                 summed[k, s] = (part[k, core, s].astype(F32) + pair[k, s].astype(F32)).astype(BF16)
-                t_copy(k, s).start()
+                for d in far:
+                    t_copy(k, s, line_peer(d)).start()
 
         return carry
 
     lax.fori_loop(0, chunks + 2, down, 0)
 
-    share_rows = weights[...].astype(BF16)
+    share_rows = jnp.transpose(weights[...]).astype(BF16)
 
     def finish(step, carry):
         @pl.when(step < chunks)
         def _():
             k = step
-            total = part[k, core, side].astype(F32) + pair[k, side].astype(F32)
-            for i in range(1, sides):
-                s = side_peer(i)
-                remote(
-                    summed.at[k, s], across.at[k, s],
-                    t_send.at[k, s], t_recv.at[k, s], at_side(s),
-                ).wait_recv()
-                total = total + across[k, s].astype(F32)
-            ready[k] = total.astype(BF16)
-            for i in range(1, experts):
-                v_copy(k, ep_peer(i)).start()
+            for d in far:
+                z = line_peer(d)
+                span = pl.ds(z * lanes, lanes)
+                total = part[k, core, side, span].astype(F32) + pair[k, side, span].astype(F32)
+                for i in range(1, sides):
+                    s = side_peer(i)
+                    t_arrival(k, s, z).wait_recv()
+                    total = total + across[k, s, span].astype(F32)
+                ready[k, span] = total.astype(BF16)
+                for b in range(lanes):
+                    if (d, b) != (0, 0):
+                        v_copy(k, ep_at(d, b)).start()
             back[k, me] = ready[k, me]
 
         @pl.when(step >= 1)
@@ -240,11 +273,12 @@
         for i in range(1, experts):
             a_copy(k, ep_peer(i)).wait_send()
             v_copy(k, ep_peer(i)).wait_send()
-        for i in range(1, sides):
-            x_copy(k, side_peer(i)).wait_send()
-            t_copy(k, side_peer(i)).wait_send()
-        for s in range(sides):
-            d_copy(k, s).wait_send()
+        for z in range(lines):
+            for i in range(1, sides):
+                x_copy(k, side_peer(i), z).wait_send()
+                t_copy(k, side_peer(i), z).wait_send()
+            for s in range(sides):
+                d_copy(k, s, z).wait_send()
         q_copy(k).wait_send()
         return carry
 
@@ -259,8 +293,9 @@
     sides = lax.axis_size("tp") // 2
     capacity = 2 * token_rows * top // experts
     pad = -(-capacity // 8) * 8
-    cut = min(512, width)
+    cut = min(1024, width)
     chunks = width // cut
+    lines = experts // 2 if experts % 2 == 0 else experts
     all_rows = 2 * sides * experts * pad
     vmem, dma = pltpu.VMEM, pltpu.SemaphoreType.DMA
     in_vmem = pl.BlockSpec(memory_space=pltpu.VMEM)
@@ -286,19 +321,19 @@
             vmem((chunks, sides) + group, BF16),
             vmem((chunks,) + group, BF16),
             vmem((chunks,) + group, BF16),
-            vmem((2 * token_rows, experts * pad), F32),
+            vmem((experts * pad, 2 * token_rows), F32),
             dma((3, chunks)),
             dma((chunks, experts)), dma((chunks, experts)),
-            dma((chunks, sides)), dma((chunks, sides)),
-            dma((chunks, sides)), dma((chunks, sides)),
+            dma((chunks, sides, lines)), dma((chunks, sides, lines)),
+            dma((chunks, sides, lines)), dma((chunks, sides, lines)),
             dma((chunks,)), dma((chunks,)),
-            dma((chunks, sides)), dma((chunks, sides)),
+            dma((chunks, sides, lines)), dma((chunks, sides, lines)),
             dma((chunks, experts)), dma((chunks, experts)),
         ],
         compiler_params=pltpu.CompilerParams(
             collective_id=0, has_side_effects=True, vmem_limit_bytes=60 * 1024 * 1024
         ),
-    )(tokens, routes, combine, gate_weight, up_weight, down_weight)
+    )(tokens, routes.T, combine.T, gate_weight, up_weight, down_weight)
 
 
 def solution(mesh):

time: 65.3 us -> 53.8 us (0.82)
  Pallas kernels: 60.9 us -> 52.1 us
  local copies, waits for them, and re-layouts: 4.27 us -> 1.57 us
    pallas_call x1, Pallas kernels: 60.9 us -> 52.1 us  [body(): pl.pallas_call(functools.partial(kernel, experts=experts, capacity=capaci...]
    unnamed x3 -> x1, local copies, waits for them, and re-layouts: 4.27 us -> 1.57 us
where the time goes in v2:
time: 53.8 us; the launch traced here: 53.7 us
  Pallas kernels  52.1 us (97%)
  local copies, waits for them, and re-layouts  1.57 us (3%)
    pallas_call x1, Pallas kernels, body(): pl.pallas_call(functools.partial(kernel, experts=experts, capacity=capaci...  52.1 us
    unnamed x1, local copies, waits for them, and re-layouts  1.57 us

profile of v2, /device:TPU:0, one launch (start us, length us, event | category | flops | bytes accessed | tf_op | source)
XLA Modules:
  0.0 53.7 jit_solution(1521810684372276170)
XLA Ops:
  0.0 52.1 %shard_map.64 = bf16[16,4096]{1,0:T(8,128)(2,1)} custom-call(bf16[16,4096]{1,0:T(8,128)(2,1)} %tokens_ref.1, s32[2,16]{1,0:T(2,128)} %bitcast.2, f32[2,16]{1,0:T(2,128)} %bitcast.3, bf16[1,4096,1024]{2,1,0:T(8,128)(2,1)} %gate_hbm.1, bf16[1,4096,1024]{2,1,0:T(8,128)(2,1)} %up_hbm.1, bf16[1,1024,4096]{2,1,0:T(8,128)(2,1)} %down_hbm.1), custom_call_target="tpu_custom_call" | custom-call | tf_op jit(solution)/shard_map/pallas_call | solution.py:304
  52.1 1.6 %copy.8 = bf16[16,4096]{1,0:T(8,128)(2,1)} copy(bf16[16,4096]{1,0:T(8,128)(2,1)} %shard_map.64) | data formatting | bytes 262144

commit v3 on v2

--- a/solution.py
+++ b/solution.py
@@ -133,11 +133,11 @@
         return remote(block, block, x_send.at[k, s, z], x_recv.at[k, s, z], at_side(s))
 
     def d_copy(k, s, z):
-        block = row_block(k, core, s, z)
+        block = rows.at[k, core, s]
         return remote(block, block, d_send.at[k, s, z], d_recv.at[k, s, z], at_mate)
 
     def d_arrival(k, s, z):
-        block = row_block(k, mate, s, z)
+        block = rows.at[k, mate, s]
         return remote(block, block, d_send.at[k, s, z], d_recv.at[k, s, z], at_mate)
 
     gate_acc[...] = jnp.zeros_like(gate_acc)
@@ -158,7 +158,7 @@
                         ).wait_recv()
                 for i in range(1, sides):
                     x_copy(k, side_peer(i), z).start()
-                d_copy(k, side, z).start()
+            d_copy(k, side, 0).start()
 
         @pl.when(jnp.logical_and(step >= 1, step < chunks + 1))
         def _():
@@ -168,7 +168,8 @@
                 for i in range(1, sides):
                     s = side_peer(i)
                     x_arrival(k, s, z).wait_recv()
-                    d_copy(k, s, z).start()
+            for i in range(1, sides):
+                d_copy(k, side_peer(i), 0).start()
 
         @pl.when(step >= 2)
         def _():
@@ -176,8 +177,7 @@
             for copy in weight_copies(k):
                 copy.wait()
             for s in range(sides):
-                for z in range(lines):
-                    d_arrival(k, s, z).wait_recv()
+                d_arrival(k, s, 0).wait_recv()
             x = rows[k].astype(F32).reshape(all_rows, cut).astype(BF16)
             gate_acc[...] += jnp.dot(x, gate_ref[k], preferred_element_type=F32)
             up_acc[...] += jnp.dot(x, up_ref[k], preferred_element_type=F32)
@@ -218,9 +218,9 @@
             part[k] = block.reshape(2, sides, experts, pad, cut).astype(BF16)
             q_copy(k).start()
 
-        @pl.when(step >= 2)
-        def _():
-            k = step - 2
+        @pl.when(step >= 1)
+        def _():
+            k = step - 1
             q_copy(k).wait_recv()
             for i in range(1, sides):
                 s = side_peer(i)
@@ -230,7 +230,7 @@
 
         return carry
 
-    lax.fori_loop(0, chunks + 2, down, 0)
+    lax.fori_loop(0, chunks + 1, down, 0)
 
     share_rows = jnp.transpose(weights[...]).astype(BF16)
 
@@ -277,8 +277,8 @@
             for i in range(1, sides):
                 x_copy(k, side_peer(i), z).wait_send()
                 t_copy(k, side_peer(i), z).wait_send()
-            for s in range(sides):
-                d_copy(k, s, z).wait_send()
+        for s in range(sides):
+            d_copy(k, s, 0).wait_send()
         q_copy(k).wait_send()
         return carry
 

time: 53.8 us -> 53.6 us (level)
  no operation moved by 1% of the time
where the time goes in v3:
time: 53.6 us; the launch traced here: 53.4 us
  Pallas kernels  51.9 us (97%)
  local copies, waits for them, and re-layouts  1.57 us (3%)
    pallas_call x1, Pallas kernels, body(): pl.pallas_call(functools.partial(kernel, experts=experts, capacity=capaci...  51.9 us
    unnamed x1, local copies, waits for them, and re-layouts  1.57 us

profile of v3, /device:TPU:0, one launch (start us, length us, event | category | flops | bytes accessed | tf_op | source)
XLA Modules:
  0.0 53.4 jit_solution(10104357330244401646)
XLA Ops:
  0.0 51.9 %shard_map.64 = bf16[16,4096]{1,0:T(8,128)(2,1)} custom-call(bf16[16,4096]{1,0:T(8,128)(2,1)} %tokens_ref.1, s32[2,16]{1,0:T(2,128)} %bitcast.2, f32[2,16]{1,0:T(2,128)} %bitcast.3, bf16[1,4096,1024]{2,1,0:T(8,128)(2,1)} %gate_hbm.1, bf16[1,4096,1024]{2,1,0:T(8,128)(2,1)} %up_hbm.1, bf16[1,1024,4096]{2,1,0:T(8,128)(2,1)} %down_hbm.1), custom_call_target="tpu_custom_call" | custom-call | tf_op jit(solution)/shard_map/pallas_call | solution.py:304
  51.9 1.6 %copy.8 = bf16[16,4096]{1,0:T(8,128)(2,1)} copy(bf16[16,4096]{1,0:T(8,128)(2,1)} %shard_map.64) | data formatting | bytes 262144
